TPU v7x, 32 devices: a whole 2x2x4 slice. The times are simulated.
32 devices in a mesh: slices: 2 (over x), wide: 4 (over y, core), narrow: 4 (over z).
Axes of the slice: x: 2, y: 2, z: 4, core: 2. Of those that a mesh axis runs over, the one named last changes fastest.
Arguments:
- state: float32 [8, 4, 2, 16384], P(('slices', 'wide'), 'narrow'), parts along dimension 0, may hold values from -6 to 6
- gates: float32 [8, 7, 2, 4, 4], replicated, may hold values from -2 to 2
Outputs:
- final_state: float32 [8, 4, 2, 16384], P(('slices', 'wide'), 'narrow'), parts along dimension 0
- marginal: float32 [8, 16384], P(('slices', 'wide'), 'narrow'), parts along dimension 0
There are 2 independent parts, one for each index of `slices`. A program takes and returns all parts, laid end to end along the dimension named above; an argument that names none is the same for every part. Nothing has to cross between parts.
All inputs are finite; a program needn't handle non-finite values.
Results may differ from a plain program's by a relative error of at most 0.0003.
Values sent between devices are 32-bit elements; how exact they have to be, the bound alone decides.
A program may use at most 192 MiB of HBM per device.

v0:
```python
import functools

import jax
import jax.numpy as jnp
from jax import lax
from jax.experimental import pallas as pl
from jax.experimental.pallas import tpu as pltpu
from jax.sharding import PartitionSpec as P


def kron_chain(members):
    real_part = members[0][0]
    imag_part = members[0][1]
    for member in members[1:]:
        other_real = member[0]
        other_imag = member[1]
        new_real = jnp.kron(real_part, other_real) - jnp.kron(imag_part, other_imag)
        new_imag = jnp.kron(real_part, other_imag) + jnp.kron(imag_part, other_real)
        real_part, imag_part = (new_real, new_imag)
    return (real_part, imag_part)


def rotate(flat, wide_count, narrow_count):
    devices = wide_count * narrow_count
    amplitudes = flat.shape[1]
    rest = amplitudes // devices
    blocks = flat.reshape(2, rest, devices)
    turned = jnp.swapaxes(blocks, 1, 2)
    moved = lax.all_to_all(turned, ("wide", "narrow"), split_axis=1, concat_axis=1, tiled=True)
    return moved.reshape(2, amplitudes)


def apply_layer(flat, layer_gates):
    amplitudes = flat.shape[1]
    pairs = layer_gates.shape[0]
    upper = amplitudes // 256
    low_real, low_imag = kron_chain([layer_gates[index] for index in range(3, -1, -1)])
    high_real, high_imag = kron_chain([layer_gates[index] for index in range(pairs - 1, 3, -1)])
    blocks = flat.reshape(2, upper, 256)
    real_rows = blocks[0]
    imag_rows = blocks[1]
    highest = lax.Precision.HIGHEST
    next_real = jnp.dot(real_rows, low_real.T, precision=highest) - jnp.dot(
        imag_rows, low_imag.T, precision=highest
    )
    next_imag = jnp.dot(real_rows, low_imag.T, precision=highest) + jnp.dot(
        imag_rows, low_real.T, precision=highest
    )
    final_real = jnp.dot(high_real, next_real, precision=highest) - jnp.dot(
        high_imag, next_imag, precision=highest
    )
    final_imag = jnp.dot(high_imag, next_real, precision=highest) + jnp.dot(
        high_real, next_imag, precision=highest
    )
    return jnp.stack([final_real, final_imag]).reshape(2, amplitudes)


MESH = pl.DeviceIdType.MESH
LANES = 128


def complex_mul(left, right):
    return (
        left[0] * right[0] - left[1] * right[1],
        left[0] * right[1] + left[1] * right[0],
    )


def merged_gates(planes, plan, which):
    layers, pairs, shift, total_pairs, _, radix = plan
    lane = lax.broadcasted_iota(jnp.int32, planes[0][0].shape, 1)
    down = lax.broadcasted_iota(jnp.int32, planes[0][0].shape, 0)
    unit = jnp.where(lane // layers == down, 1.0, 0.0)
    unit = (unit, jnp.zeros_like(unit))
    items = []
    for layer in range(layers):
        places = [(pair - layer * shift) % total_pairs for pair in which]
        chosen = [planes[place] if place < pairs else unit for place in places]
        items.append((tuple(jnp.stack([gate[c] for gate in chosen]) for c in range(2)), layer))
    while len(items) > 1:
        joined = []
        for at in range(0, len(items) - 1, 2):
            (early, last), (late, newest) = items[at], items[at + 1]
            total = None
            for row in range(radix):
                lane_at = row * layers + last
                term = complex_mul(
                    tuple(part[:, :, lane_at : lane_at + 1] for part in early),
                    tuple(part[:, row : row + 1, :] for part in late),
                )
                total = term if total is None else (total[0] + term[0], total[1] + term[1])
            joined.append((total, newest))
        if len(items) % 2:
            joined.append(items[-1])
        items = joined
    parts, last = items[0]
    return [(tuple(part[index] for part in parts), last) for index in range(len(which))]


def kron_all(members, layers):
    radix = members[0][0][0].shape[0]
    size = radix ** len(members)
    lane = lax.broadcasted_iota(jnp.int32, (1, size), 1)
    rows = None
    for place, (member, last) in enumerate(reversed(members)):
        field = (lane // radix**place) % radix
        wide = []
        for part in member:
            columns = [part[:, index * layers + last : index * layers + last + 1] for index in range(radix)]
            spread = jnp.broadcast_to(columns[-1], (radix, size))
            for index in range(radix - 1):
                spread = jnp.where(field == index, columns[index], spread)
            wide.append(spread)
        if rows is None:
            rows = tuple(wide)
            continue
        pieces = [
            complex_mul(tuple(part[index : index + 1, :] for part in wide), rows)
            for index in range(radix)
        ]
        rows = tuple(jnp.concatenate([piece[c] for piece in pieces], axis=0) for c in range(2))
    return rows


def split(value):
    high = value.astype(jnp.bfloat16)
    return high, (value - high.astype(jnp.float32)).astype(jnp.bfloat16)


def dot(left, right, contract):
    def one(a, b):
        return lax.dot_general(a, b, (((1,), (contract,)), ((), ())), preferred_element_type=jnp.float32)

    return one(left[0], right[0]) + (one(left[0], right[1]) + one(left[1], right[0]))


def exchange_kernel(plan, x_hbm, g_hbm, recv, lane_hi, lane_lo, row_hi, row_lo, x, g, send,
                    local_sem, send_sem, recv_sem):
    layers, pairs, shift, total_pairs, start, radix = plan
    w = lax.axis_index("wide")
    n = lax.axis_index("narrow")
    offsets = [(dw, dn) for dw in range(radix) for dn in range(radix) if dw or dn]

    def partner(dw, dn):
        return lax.rem(w + dw, radix), lax.rem(n + dn, radix)

    barrier = pltpu.get_barrier_semaphore()
    copy_g = pltpu.make_async_copy(g_hbm, g, local_sem.at[0])
    copy_x = pltpu.make_async_copy(x_hbm, x, local_sem.at[1])
    copy_g.start()
    copy_x.start()
    for dw, dn in offsets:
        pw, pn = partner(dw, dn)
        pl.semaphore_signal(barrier, inc=1, device_id={"wide": pw, "narrow": pn}, device_id_type=MESH)
    copy_g.wait()

    planes = []
    for index in range(pairs):
        plane = []
        for c in range(2):
            total = None
            for row in range(radix):
                tile = g[(index * 2 + c) * radix + row]
                tile = jnp.concatenate([tile, jnp.zeros((radix, LANES - layers), jnp.float32)], axis=1)
                tile = pltpu.roll(tile, row * layers, 1) if row else tile
                total = tile if total is None else total + tile
            plane.append(total)
        planes.append(tuple(plane))
    split_gate, low_gate, high_gate = merged_gates(planes, plan, range(start - 1, start + 2))

    half = LANES // 2
    group = half // radix
    rows_hi = send.shape[1] * radix // (2 * radix - 1)
    tail = rows_hi // radix
    shape = (rows_hi, LANES)
    lane = lax.broadcasted_iota(jnp.int32, shape, 1)
    first = lane < half
    field = (lane // group) % radix
    outer = lane // (2 * group)

    def entry(gate, row, column):
        lane_at = row * layers + gate[1]
        return tuple(
            jnp.broadcast_to(item[column : column + 1, lane_at : lane_at + 1], shape) for item in gate[0]
        )

    def both(gate, one, other):
        return tuple(jnp.where(first, a, b) for a, b in zip(entry(gate, *one), entry(gate, *other)))

    def add(total, term):
        return term if total is None else (total[0] + term[0], total[1] + term[1])

    def roll(value, amount):
        amount %= LANES
        return pltpu.roll(value, amount, 1) if amount else value

    steps = {}
    for row in range(radix):
        for column in range(radix):
            item = tuple(jnp.where(field == row, part, 0.0) for part in entry(split_gate, row, column))
            steps[column - row] = add(steps.get(column - row), item)

    copy_x.wait()
    same = [[both(low_gate, (2 * o, 2 * i), (2 * o + 1, 2 * i + 1)) for i in range(2)] for o in range(2)]
    cross = [[both(low_gate, (2 * o, 2 * i + 1), (2 * o + 1, 2 * i)) for i in range(2)] for o in range(2)]
    stage = []
    stride = 4 * radix
    for high in range(radix):
        held = []
        for i in range(2):
            held.append(tuple(x[pl.ds(high * 4 + i * 2 + c, rows_hi, stride=stride), :] for c in range(2)))
        turned = [tuple(roll(v, half) for v in pair) for pair in held]
        result = []
        for o in range(2):
            total = None
            for i in range(2):
                total = add(total, complex_mul(same[o][i], held[i]))
                total = add(total, complex_mul(cross[o][i], turned[i]))
            result.append(total)
        stage.append(result)
    for out_high in range(radix):
        coefs = [entry(high_gate, out_high, high) for high in range(radix)]
        ready = []
        for o in range(2):
            total = None
            for high in range(radix):
                total = add(total, complex_mul(coefs[high], stage[high][o]))
            mixed = None
            for step, coef in steps.items():
                mixed = add(mixed, complex_mul(coef, tuple(roll(v, -group * step) for v in total)))
            ready.append(mixed)
            rolled = tuple(roll(v, half) for v in mixed)
            at = out_high * radix + 2 * o
            send[at, :rows_hi] = jnp.where(first, mixed[0], rolled[1])
            send[at + 1, :rows_hi] = jnp.where(first, rolled[0], mixed[1])
        for take in range(radix):
            block = None
            for o in range(2):
                for c in range(2):
                    piece = roll(ready[o][c], (2 * o + c - take) * group)
                    block = piece if block is None else jnp.where(field == 2 * o + c, piece, block)
            spare = (take % 2) * 2 + take // 2
            if spare != radix - 1:
                block = jnp.where(outer == spare, roll(block, 2 * group * (spare + 1)), block)
            moved = [roll(block[rows_hi - tail :], -2 * group * (k + 1)) for k in range(radix - 1)]
            send[out_high * radix + take, rows_hi:] = jnp.where(
                outer[: rows_hi - tail] == radix - 1,
                jnp.concatenate(moved, axis=0),
                block[: rows_hi - tail],
            )

    pl.semaphore_wait(barrier, len(offsets))
    me = w * radix + n
    count = radix * radix
    seat = ((radix - n) % radix) * radix + w
    copies = []
    for at in range(count - 1):
        other = at + (at + count - seat) // count
        pw, pn = other % radix, (radix - other // radix) % radix
        copy = pltpu.make_async_remote_copy(
            src_ref=send.at[pw * radix + pn],
            dst_ref=recv.at[me],
            send_sem=send_sem.at[other],
            recv_sem=recv_sem.at[seat],
            device_id={"wide": pw, "narrow": pn},
            device_id_type=MESH,
        )
        copy.start()
        copies.append(copy)
    recv[me] = send[me]

    rest = list(range(start - 1)) + list(range(start + 2, total_pairs))
    rest = dict(zip(rest, merged_gates(planes, plan, rest)))
    low = kron_all([rest[pair] for pair in range(start - 2, -1, -1)], layers)
    block = jnp.concatenate(
        [jnp.concatenate([low[0], low[1]], axis=1), jnp.concatenate([-low[1], low[0]], axis=1)], axis=0
    )
    block = jnp.concatenate([jnp.concatenate([block] * radix, axis=0)] * radix, axis=1)
    down = lax.broadcasted_iota(jnp.int32, (LANES, LANES), 0)
    across = lax.broadcasted_iota(jnp.int32, (LANES, LANES), 1)
    grouped = jnp.where(down // (2 * group) == across // (2 * group), block, 0.0).T
    parts = [jnp.concatenate([jnp.concatenate([item] * radix, axis=0)] * radix, axis=1) for item in low]
    keep = (down[:half, :half] // group) == (across[:half, :half] // group)
    parts = [jnp.where(keep, item, 0.0) for item in parts]
    plain = jnp.concatenate(
        [jnp.concatenate([parts[0], parts[1]], axis=1), jnp.concatenate([-parts[1], parts[0]], axis=1)],
        axis=0,
    ).T
    for index, item in enumerate((plain, grouped)):
        lane_hi[index], lane_lo[index] = split(item)
    row_members = [rest[pair] for pair in range(total_pairs - 1, start + 1, -1)]
    for index, item in enumerate(kron_all(row_members, layers)):
        row_hi[index], row_lo[index] = split(item)

    for copy in copies:
        copy.wait_send()
    for at in range(count - 1):
        other = at + (at + count - seat) // count
        pw, pn = other % radix, (radix - other // radix) % radix
        pltpu.make_async_remote_copy(
            src_ref=send.at[me],
            dst_ref=recv.at[pw * radix + pn],
            send_sem=send_sem.at[other],
            recv_sem=recv_sem.at[other],
            device_id={"wide": pw, "narrow": pn},
            device_id_type=MESH,
        ).wait_recv()


def finish_kernel(radix, recv, lane_hi, lane_lo, row_hi, row_lo, out_hbm, marg_hbm, fin, prob, marg, sems):
    rows_hi = recv.shape[1] * radix // (2 * radix - 1)
    tail = rows_hi // radix
    size = recv.shape[0] * rows_hi
    half = LANES // 2
    group = half // radix
    blocks = size // LANES
    rows = (row_hi[0], row_lo[0]), (row_hi[1], row_lo[1])

    def apply(which, value, keep):
        held = split(value.reshape(size, LANES))
        turned = dot((lane_hi[which], lane_lo[which]), held, 1)
        turned = split(turned[:keep])
        return dot(turned, rows[0], 0), dot(turned, rows[1], 0)

    with_real, with_imag = apply(0, recv[:, :rows_hi], LANES)
    real = with_real[:half] - with_imag[half:]
    imag = with_real[half:] + with_imag[:half]
    for block in range(blocks):
        columns = slice(block * LANES, (block + 1) * LANES)
        fin[pl.ds(block * 2, half, stride=2 * blocks), :] = real[:, columns]
        fin[pl.ds(block * 2 + 1, half, stride=2 * blocks), :] = imag[:, columns]
    out_copy = pltpu.make_async_copy(fin, out_hbm, sems.at[0])
    out_copy.start()
    density = real * real + imag * imag
    for index in range(radix):
        prob[index] = density[index * group : (index + 1) * group]
    packed = recv[:, rows_hi:]
    outer = lax.broadcasted_iota(jnp.int32, (1, tail, LANES), 2) // (2 * group)
    last = None
    for index in range(radix - 1):
        piece = packed[:, index * tail : (index + 1) * tail]
        piece = pltpu.roll(piece, 2 * group * (index + 1), 2)
        last = piece if last is None else jnp.where(outer == index, piece, last)
    wide = jnp.concatenate([packed, last], axis=1)
    with_real, with_imag = apply(1, wide, LANES - 2 * group)
    total = prob[lax.axis_index("narrow")]
    for index in range(radix - 1):
        at = 2 * group * index
        real = with_real[at : at + group] - with_imag[at + group : at + 2 * group]
        imag = with_real[at + group : at + 2 * group] + with_imag[at : at + group]
        term = real * real + imag * imag
        total = total + term
    for block in range(blocks):
        marg[pl.ds(block, group, stride=blocks), :] = total[:, block * LANES : (block + 1) * LANES]
    marg_copy = pltpu.make_async_copy(marg, marg_hbm, sems.at[1])
    marg_copy.start()
    out_copy.wait()
    marg_copy.wait()


def window_plan(wide_count, narrow_count, amplitudes, gates_shape):
    layers, pairs, radix = gates_shape[0], gates_shape[1], gates_shape[-1]
    high_bits = (wide_count * narrow_count).bit_length() - 1
    local_bits = amplitudes.bit_length() - 1
    total_bits = high_bits + local_bits
    if high_bits % 2 or local_bits % 2 or wide_count != radix or narrow_count != radix:
        return None
    if 2 * pairs != local_bits:
        return None
    offset = ((layers - 1) * high_bits) % total_bits
    start = offset // 2 - high_bits // 2
    if layers * radix > LANES or start < 2 or offset // 2 >= pairs or 2 * radix**start != LANES:
        return None
    rows_hi = radix ** (pairs - offset // 2)
    if rows_hi % 8:
        return None
    for which in range(total_bits // 2):
        if all((which - layer * (high_bits // 2)) % (total_bits // 2) >= pairs for layer in range(layers)):
            return None
    return (layers, pairs, high_bits // 2, total_bits // 2, start, radix), rows_hi


def merged_local(plan, rows_hi, state, gates):
    radix = plan[-1]
    amplitudes = state.shape[-1]
    rows = amplitudes // LANES
    count = radix * radix
    own = amplitudes // radix // LANES
    x = jnp.swapaxes(state.reshape(2, rows, LANES), 0, 1).reshape(2 * rows, LANES)
    g = jnp.transpose(gates, (1, 2, 3, 4, 0)).reshape(-1, radix, gates.shape[0])
    f32, bf16 = jnp.float32, jnp.bfloat16
    size = count * rows_hi
    message = 2 * rows_hi - rows_hi // radix
    shared = (
        pltpu.VMEM((count, message, LANES), f32),
        pltpu.VMEM((2, LANES, LANES), bf16),
        pltpu.VMEM((2, LANES, LANES), bf16),
        pltpu.VMEM((2, size, size), bf16),
        pltpu.VMEM((2, size, size), bf16),
    )
    held = pl.pallas_call(
        functools.partial(exchange_kernel, plan),
        out_shape=shared,
        in_specs=[pl.BlockSpec(memory_space=pltpu.HBM)] * 2,
        out_specs=[pl.BlockSpec(memory_space=pltpu.VMEM)] * len(shared),
        scratch_shapes=[
            pltpu.VMEM(x.shape, f32),
            pltpu.VMEM(g.shape, f32),
            pltpu.VMEM((count, message, LANES), f32),
            pltpu.SemaphoreType.DMA((2,)),
            pltpu.SemaphoreType.DMA((count,)),
            pltpu.SemaphoreType.DMA((count,)),
        ],
        compiler_params=pltpu.CompilerParams(
            collective_id=0, has_side_effects=True, vmem_limit_bytes=8 * 2**20
        ),
        name="exchange",
    )(
        pltpu.with_memory_space_constraint(x, pltpu.HBM),
        pltpu.with_memory_space_constraint(g, pltpu.HBM),
    )
    out, marg = pl.pallas_call(
        functools.partial(finish_kernel, radix),
        out_shape=(pltpu.HBM((2 * rows, LANES), f32), pltpu.HBM((own, LANES), f32)),
        in_specs=[pl.BlockSpec(memory_space=pltpu.VMEM)] * len(shared),
        out_specs=[pl.BlockSpec(memory_space=pltpu.HBM)] * 2,
        scratch_shapes=[
            pltpu.VMEM((2 * rows, LANES), f32),
            pltpu.VMEM((radix, LANES // 2 // radix, size), f32),
            pltpu.VMEM((own, LANES), f32),
            pltpu.SemaphoreType.DMA((2,)),
        ],
        compiler_params=pltpu.CompilerParams(vmem_limit_bytes=8 * 2**20),
        name="finish",
    )(*held)
    final = jnp.swapaxes(out.reshape(rows, 2, LANES), 0, 1).reshape(1, 1, 2, amplitudes)
    return final, marg.reshape(1, -1)


def local(state, gates):
    wide_count = lax.axis_size("wide")
    narrow_count = lax.axis_size("narrow")
    amplitudes = state.shape[-1]
    found = window_plan(wide_count, narrow_count, amplitudes, gates.shape)
    if found is not None:
        return merged_local(*found, state, gates)
    flat = state.reshape(2, amplitudes)
    for layer_index in range(gates.shape[0]):
        if layer_index > 0:
            flat = rotate(flat, wide_count, narrow_count)
        flat = apply_layer(flat, gates[layer_index])
    prob = flat[0] * flat[0] + flat[1] * flat[1]
    marginal = lax.psum_scatter(prob, "narrow", scatter_dimension=0, tiled=True)
    return (flat.reshape(1, 1, 2, amplitudes), marginal.reshape(1, -1))


def solution(mesh):
    in_specs = (P(("slices", "wide"), "narrow", None, None), P())
    out_specs = (P(("slices", "wide"), "narrow", None, None), P(("slices", "wide"), "narrow"))
    return jax.shard_map(local, mesh=mesh, in_specs=in_specs, out_specs=out_specs, check_vma=False)
```

profile of v0, /device:TPU:0, one launch (start us, length us, event | category | flops | bytes accessed | tf_op | source)
XLA Modules:
  0.0 13.7 jit_solution(366415809514730823)
XLA Ops:
  0.6 11.8 %exchange.1 = (f32[16,28,128]{2,1,0:T(8,128)S(1)}, bf16[2,128,128]{2,1,0:T(8,128)(2,1)S(1)}, bf16[2,128,128]{2,1,0:T(8,128)(2,1)S(1)}, bf16[2,256,256]{2,1,0:T(8,128)(2,1)S(1)}, bf16[2,256,256]{2,1,0:T(8,128)(2,1)S(1)}) custom-call(f32[256,128]{1,0:T(8,128)} %bitcast.14, f32[56,4,8]{2,1,0:T(4,128)} %bitcast.15), custom_call_target="tpu_custom_call" | custom-call | tf_op jit(solution)/shard_map/exchange/pallas_call | solution.py:401
  12.5 1.2 %finish.1 = (f32[256,128]{1,0:T(8,128)}, f32[32,128]{1,0:T(8,128)}) custom-call(f32[16,28,128]{2,1,0:T(8,128)S(1)} %get-tuple-element.9.recv, bf16[2,128,128]{2,1,0:T(8,128)(2,1)S(1)} %get-tuple-element.10.lane_hi, bf16[2,128,128]{2,1,0:T(8,128)(2,1)S(1)} %get-tuple-element.11.lane_lo, bf16[2,256,256]{2,1,0:T(8,128)(2,1)S(1)} %get-tuple-element.12.row_hi, ...), custom_call_target="tpu_custom_call" | custom-call | tf_op jit(solution)/shard_map/finish/pallas_call | solution.py:422
where the time goes:
time: 13.9 us; the launch traced here: 13.7 us
  Pallas kernels  13.1 us (94%)
  between operations  0.64 us (5%)
    pallas_call x1, Pallas kernels, merged_local(): pl.pallas_call(functools.partial(exchange_kernel, plan), out_shape=shared...  11.8 us
    pallas_call x1, Pallas kernels, merged_local(): pl.pallas_call(functools.partial(finish_kernel, radix), out_shape=(pltpu....  1.24 us

commit v1 on v0

--- a/solution.py
+++ b/solution.py
@@ -66,60 +66,79 @@
     )
 
 
-def merged_gates(planes, plan, which):
+def merged_gates(g, plan, order):
     layers, pairs, shift, total_pairs, _, radix = plan
-    lane = lax.broadcasted_iota(jnp.int32, planes[0][0].shape, 1)
-    down = lax.broadcasted_iota(jnp.int32, planes[0][0].shape, 0)
-    unit = jnp.where(lane // layers == down, 1.0, 0.0)
-    unit = (unit, jnp.zeros_like(unit))
-    items = []
-    for layer in range(layers):
-        places = [(pair - layer * shift) % total_pairs for pair in which]
-        chosen = [planes[place] if place < pairs else unit for place in places]
-        items.append((tuple(jnp.stack([gate[c] for gate in chosen]) for c in range(2)), layer))
-    while len(items) > 1:
-        joined = []
-        for at in range(0, len(items) - 1, 2):
-            (early, last), (late, newest) = items[at], items[at + 1]
-            total = None
-            for row in range(radix):
-                lane_at = row * layers + last
-                term = complex_mul(
-                    tuple(part[:, :, lane_at : lane_at + 1] for part in early),
-                    tuple(part[:, row : row + 1, :] for part in late),
-                )
-                total = term if total is None else (total[0] + term[0], total[1] + term[1])
-            joined.append((total, newest))
-        if len(items) % 2:
-            joined.append(items[-1])
-        items = joined
-    parts, last = items[0]
-    return [(tuple(part[index] for part in parts), last) for index in range(len(which))]
-
-
-def kron_all(members, layers):
-    radix = members[0][0][0].shape[0]
+    shape = (2 * radix, LANES)
+    lane = lax.broadcasted_iota(jnp.int32, shape, 1)
+    down = lax.broadcasted_iota(jnp.int32, shape, 0)
+    slots = LANES // (radix * layers)
+    layer, row, slot = lane % layers, (lane // layers) % radix, lane // (radix * layers)
+    pad = jnp.zeros((radix, LANES - layers), jnp.float32)
+    planes = []
+    for pair in range(pairs):
+        plane = None
+        for at in range(radix):
+            tile = jnp.concatenate(
+                [jnp.concatenate([g[(pair * 2 + c) * radix + at], pad], axis=1) for c in range(2)], axis=0
+            )
+            tile = jnp.take_along_axis(tile, layer, axis=1, mode="promise_in_bounds")
+            plane = tile if plane is None else jnp.where(row == at, tile, plane)
+        planes.append(plane)
+    unit = jnp.where(down == row, 1.0, 0.0)
+    sign = jnp.where(down < radix, -1.0, 1.0)
+    found = {}
+    for begin in range(0, len(order), slots):
+        held = order[begin : begin + slots]
+        place = held[0] - shift * layer
+        for index, pair in enumerate(held[1:]):
+            place = jnp.where(slot == index + 1, pair - shift * layer, place)
+        for _ in range(-(-layers * shift // total_pairs)):
+            place = jnp.where(place < 0, place + total_pairs, place)
+        total = unit
+        for pair in range(pairs):
+            total = jnp.where(place == pair, planes[pair], total)
+        step = 1
+        while step < layers:
+            source = slot * (radix * layers) + jnp.maximum(layer - step, 0)
+            straight, crossed = None, None
+            for at in range(radix):
+                early = jnp.take_along_axis(total, source + at * layers, axis=1, mode="promise_in_bounds")
+                one = total[at : at + 1] * early
+                two = total[radix + at : radix + at + 1] * early
+                straight = one if straight is None else straight + one
+                crossed = two if crossed is None else crossed + two
+            total = straight + sign * pltpu.roll(crossed, radix, 0)
+            step *= 2
+        for index, pair in enumerate(held):
+            found[pair] = [
+                jnp.broadcast_to(total[:, at : at + 1], shape)
+                for at in range(index * radix * layers + layers - 1, (index + 1) * radix * layers, layers)
+            ]
+    return found
+
+
+def kron_all(members):
+    radix = len(members[0])
     size = radix ** len(members)
-    lane = lax.broadcasted_iota(jnp.int32, (1, size), 1)
+    width = max(size, LANES)
+    lane = lax.broadcasted_iota(jnp.int32, (2 * radix, width), 1)
     rows = None
-    for place, (member, last) in enumerate(reversed(members)):
+    for place, member in enumerate(reversed(members)):
         field = (lane // radix**place) % radix
-        wide = []
-        for part in member:
-            columns = [part[:, index * layers + last : index * layers + last + 1] for index in range(radix)]
-            spread = jnp.broadcast_to(columns[-1], (radix, size))
-            for index in range(radix - 1):
-                spread = jnp.where(field == index, columns[index], spread)
-            wide.append(spread)
+        columns = [jnp.concatenate([column] * (width // LANES), axis=1) for column in member]
+        spread = columns[-1]
+        for index in range(radix - 1):
+            spread = jnp.where(field == index, columns[index], spread)
+        wide = spread[:radix], spread[radix:]
         if rows is None:
-            rows = tuple(wide)
+            rows = wide
             continue
         pieces = [
             complex_mul(tuple(part[index : index + 1, :] for part in wide), rows)
             for index in range(radix)
         ]
         rows = tuple(jnp.concatenate([piece[c] for piece in pieces], axis=0) for c in range(2))
-    return rows
+    return tuple(part[:, :size] for part in rows)
 
 
 def split(value):
@@ -134,43 +153,47 @@
     return one(left[0], right[0]) + (one(left[0], right[1]) + one(left[1], right[0]))
 
 
+def greet(semaphore, seat, level):
+    pl.semaphore_signal(semaphore, inc=1, device_id={"wide": seat, "narrow": level}, device_id_type=MESH)
+
+
 def exchange_kernel(plan, x_hbm, g_hbm, recv, lane_hi, lane_lo, row_hi, row_lo, x, g, send,
-                    local_sem, send_sem, recv_sem):
+                    local_sem, send_sem, recv_sem, known):
     layers, pairs, shift, total_pairs, start, radix = plan
     w = lax.axis_index("wide")
     n = lax.axis_index("narrow")
-    offsets = [(dw, dn) for dw in range(radix) for dn in range(radix) if dw or dn]
-
-    def partner(dw, dn):
-        return lax.rem(w + dw, radix), lax.rem(n + dn, radix)
+    me = n * radix + w
+    count = radix * radix
 
     barrier = pltpu.get_barrier_semaphore()
     copy_g = pltpu.make_async_copy(g_hbm, g, local_sem.at[0])
     copy_x = pltpu.make_async_copy(x_hbm, x, local_sem.at[1])
     copy_g.start()
     copy_x.start()
-    for dw, dn in offsets:
-        pw, pn = partner(dw, dn)
-        pl.semaphore_signal(barrier, inc=1, device_id={"wide": pw, "narrow": pn}, device_id_type=MESH)
+    row, core = lax.div(w, 2), lax.rem(w, 2)
+    other = 2 * (1 - row)
+    seats = [other + core, other + 1 - core, 2 * row + 1 - core, w]
+    for level in range(radix):
+        @pl.when(level >= n)
+        def _():
+            for seat in seats[:-1]:
+                greet(barrier, seat, level)
+
+            @pl.when(level != n)
+            def _():
+                greet(barrier, w, level)
+
     copy_g.wait()
-
-    planes = []
-    for index in range(pairs):
-        plane = []
-        for c in range(2):
-            total = None
-            for row in range(radix):
-                tile = g[(index * 2 + c) * radix + row]
-                tile = jnp.concatenate([tile, jnp.zeros((radix, LANES - layers), jnp.float32)], axis=1)
-                tile = pltpu.roll(tile, row * layers, 1) if row else tile
-                total = tile if total is None else total + tile
-            plane.append(total)
-        planes.append(tuple(plane))
-    split_gate, low_gate, high_gate = merged_gates(planes, plan, range(start - 1, start + 2))
+    copy_x.wait()
+
+    order = list(range(start - 1, start + 2)) + list(range(start - 1)) + list(range(start + 2, total_pairs))
+    gate = merged_gates(g, plan, order)
+    split_gate, low_gate, high_gate = (gate[pair] for pair in range(start - 1, start + 2))
 
     half = LANES // 2
     group = half // radix
-    rows_hi = send.shape[1] * radix // (2 * radix - 1)
+    rows_all = send.shape[1]
+    rows_hi = rows_all * radix // (2 * radix - 1)
     tail = rows_hi // radix
     shape = (rows_hi, LANES)
     lane = lax.broadcasted_iota(jnp.int32, shape, 1)
@@ -179,9 +202,8 @@
     outer = lane // (2 * group)
 
     def entry(gate, row, column):
-        lane_at = row * layers + gate[1]
         return tuple(
-            jnp.broadcast_to(item[column : column + 1, lane_at : lane_at + 1], shape) for item in gate[0]
+            jnp.broadcast_to(gate[row][at : at + 1], shape) for at in (column, column + radix)
         )
 
     def both(gate, one, other):
@@ -194,13 +216,6 @@
         amount %= LANES
         return pltpu.roll(value, amount, 1) if amount else value
 
-    steps = {}
-    for row in range(radix):
-        for column in range(radix):
-            item = tuple(jnp.where(field == row, part, 0.0) for part in entry(split_gate, row, column))
-            steps[column - row] = add(steps.get(column - row), item)
-
-    copy_x.wait()
     same = [[both(low_gate, (2 * o, 2 * i), (2 * o + 1, 2 * i + 1)) for i in range(2)] for o in range(2)]
     cross = [[both(low_gate, (2 * o, 2 * i + 1), (2 * o + 1, 2 * i)) for i in range(2)] for o in range(2)]
     stage = []
@@ -218,60 +233,121 @@
                 total = add(total, complex_mul(cross[o][i], turned[i]))
             result.append(total)
         stage.append(result)
-    for out_high in range(radix):
+    sign = jnp.where(field % 2 == 0, -1.0, 1.0)
+    mixers = [[entry(split_gate, take, f) for f in range(radix)] for take in range(radix)]
+    mixers = [[(re, im * sign) for re, im in line] for line in mixers]
+
+    def merged(out_high):
         coefs = [entry(high_gate, out_high, high) for high in range(radix)]
-        ready = []
+        held = []
         for o in range(2):
             total = None
             for high in range(radix):
                 total = add(total, complex_mul(coefs[high], stage[high][o]))
-            mixed = None
-            for step, coef in steps.items():
-                mixed = add(mixed, complex_mul(coef, tuple(roll(v, -group * step) for v in total)))
-            ready.append(mixed)
-            rolled = tuple(roll(v, half) for v in mixed)
-            at = out_high * radix + 2 * o
-            send[at, :rows_hi] = jnp.where(first, mixed[0], rolled[1])
-            send[at + 1, :rows_hi] = jnp.where(first, rolled[0], mixed[1])
-        for take in range(radix):
-            block = None
-            for o in range(2):
-                for c in range(2):
-                    piece = roll(ready[o][c], (2 * o + c - take) * group)
-                    block = piece if block is None else jnp.where(field == 2 * o + c, piece, block)
-            spare = (take % 2) * 2 + take // 2
-            if spare != radix - 1:
-                block = jnp.where(outer == spare, roll(block, 2 * group * (spare + 1)), block)
-            moved = [roll(block[rows_hi - tail :], -2 * group * (k + 1)) for k in range(radix - 1)]
-            send[out_high * radix + take, rows_hi:] = jnp.where(
-                outer[: rows_hi - tail] == radix - 1,
-                jnp.concatenate(moved, axis=0),
-                block[: rows_hi - tail],
-            )
-
-    pl.semaphore_wait(barrier, len(offsets))
-    me = w * radix + n
-    count = radix * radix
-    seat = ((radix - n) % radix) * radix + w
-    copies = []
-    for at in range(count - 1):
-        other = at + (at + count - seat) // count
-        pw, pn = other % radix, (radix - other // radix) % radix
-        copy = pltpu.make_async_remote_copy(
-            src_ref=send.at[pw * radix + pn],
+            held.append(total)
+        return held
+
+    def transposed(held):
+        turned = {}
+        for o in range(2):
+            for c in range(2):
+                for d in range(2 * o - 3, 2 * o + 2):
+                    turned[o, c, d] = roll(held[o][c], d * group)
+        blocks = []
+        for f in range(radix):
+            pair = []
+            for flip in range(2):
+                block = None
+                for o in range(2):
+                    for c in range(2):
+                        piece = turned[o, c ^ flip, 2 * o + c - f]
+                        block = piece if block is None else jnp.where(field == 2 * o + c, piece, block)
+                pair.append(block)
+            blocks.append(pair)
+        return blocks
+
+    def put(out_high, held, blocks, take):
+        real, imag = held[take // 2]
+        if take % 2:
+            main = jnp.where(first, roll(real, half), imag)
+        else:
+            main = jnp.where(first, real, roll(imag, half))
+        send[out_high * radix + take, :rows_hi] = main
+        block = None
+        for f in range(radix):
+            re, im = mixers[take][f]
+            term = re * blocks[f][0] + im * blocks[f][1]
+            block = term if block is None else block + term
+        spare = (take % 2) * 2 + take // 2
+        if spare != radix - 1:
+            block = jnp.where(outer == spare, roll(block, 2 * group * (spare + 1)), block)
+        moved = [roll(block[rows_hi - tail :], -2 * group * (k + 1)) for k in range(radix - 1)]
+        send[out_high * radix + take, rows_hi:] = jnp.where(
+            outer[: rows_hi - tail] == radix - 1,
+            jnp.concatenate(moved, axis=0),
+            block[: rows_hi - tail],
+        )
+
+    def post(seat, level):
+        pltpu.make_async_remote_copy(
+            src_ref=send.at[seat * radix + level],
             dst_ref=recv.at[me],
-            send_sem=send_sem.at[other],
-            recv_sem=recv_sem.at[seat],
-            device_id={"wide": pw, "narrow": pn},
+            send_sem=send_sem,
+            recv_sem=recv_sem.at[n],
+            device_id={"wide": seat, "narrow": level},
             device_id_type=MESH,
-        )
-        copy.start()
-        copies.append(copy)
-    recv[me] = send[me]
-
-    rest = list(range(start - 1)) + list(range(start + 2, total_pairs))
-    rest = dict(zip(rest, merged_gates(planes, plan, rest)))
-    low = kron_all([rest[pair] for pair in range(start - 2, -1, -1)], layers)
+        ).start()
+
+    def lowest(seat):
+        @pl.when((n > 0) | (w != seat))
+        def _():
+            post(seat, 0)
+
+    def below(level, carry):
+        for seat in seats:
+            post(seat, level)
+        return carry
+
+    def above(level, carry):
+        pl.semaphore_wait(known.at[level], 1)
+        return below(level, carry)
+
+    early = {}
+    for out_high in range(2):
+        held = merged(out_high)
+        early[out_high] = held, transposed(held)
+        put(out_high, *early[out_high], 0)
+
+    pl.semaphore_wait(barrier, radix * (n + 1) - 1)
+    for seat in range(2):
+        lowest(seat)
+    for level in range(radix - 1):
+        @pl.when(n > level)
+        def _():
+            greet(known.at[n], w, level)
+
+    for out_high in (2, 3, 0, 1):
+        if out_high in early:
+            held, blocks = early[out_high]
+        else:
+            held = merged(out_high)
+            blocks = transposed(held)
+        for take in range(1 if out_high in early else 0, radix):
+            put(out_high, held, blocks, take)
+
+    for seat in range(2, radix):
+        lowest(seat)
+    lax.fori_loop(1, n, below, 0)
+
+    @pl.when(n > 0)
+    def _():
+        for seat in seats[:-1]:
+            post(seat, n)
+
+    lax.fori_loop(n + 1, radix, above, 0)
+    recv[me] = send[w * radix + n]
+
+    low = kron_all([gate[pair] for pair in range(start - 2, -1, -1)])
     block = jnp.concatenate(
         [jnp.concatenate([low[0], low[1]], axis=1), jnp.concatenate([-low[1], low[0]], axis=1)], axis=0
     )
@@ -279,32 +355,35 @@
     down = lax.broadcasted_iota(jnp.int32, (LANES, LANES), 0)
     across = lax.broadcasted_iota(jnp.int32, (LANES, LANES), 1)
     grouped = jnp.where(down // (2 * group) == across // (2 * group), block, 0.0).T
-    parts = [jnp.concatenate([jnp.concatenate([item] * radix, axis=0)] * radix, axis=1) for item in low]
-    keep = (down[:half, :half] // group) == (across[:half, :half] // group)
-    parts = [jnp.where(keep, item, 0.0) for item in parts]
+    parts = kron_all([gate[pair] for pair in range(start - 1, -1, -1)])
     plain = jnp.concatenate(
         [jnp.concatenate([parts[0], parts[1]], axis=1), jnp.concatenate([-parts[1], parts[0]], axis=1)],
         axis=0,
     ).T
     for index, item in enumerate((plain, grouped)):
         lane_hi[index], lane_lo[index] = split(item)
-    row_members = [rest[pair] for pair in range(total_pairs - 1, start + 1, -1)]
-    for index, item in enumerate(kron_all(row_members, layers)):
-        row_hi[index], row_lo[index] = split(item)
-
-    for copy in copies:
-        copy.wait_send()
-    for at in range(count - 1):
-        other = at + (at + count - seat) // count
-        pw, pn = other % radix, (radix - other // radix) % radix
-        pltpu.make_async_remote_copy(
-            src_ref=send.at[me],
-            dst_ref=recv.at[pw * radix + pn],
-            send_sem=send_sem.at[other],
-            recv_sem=recv_sem.at[other],
-            device_id={"wide": pw, "narrow": pn},
+    row_members = [gate[pair] for pair in range(total_pairs - 1, start + 1, -1)]
+    for index, item in enumerate(kron_all(row_members)):
+        for at, held in enumerate(split(item)):
+            into = (row_hi, row_lo)[at]
+            for source in range(count):
+                place = (source % radix) * radix + source // radix
+                into[index, place * rows_hi : (place + 1) * rows_hi] = held[source * rows_hi : (source + 1) * rows_hi]
+
+    def settled(group, size):
+        return pltpu.make_async_remote_copy(
+            src_ref=send.at[pl.ds(0, size)],
+            dst_ref=recv.at[pl.ds(0, size)],
+            send_sem=send_sem,
+            recv_sem=recv_sem.at[group],
+            device_id={"wide": w, "narrow": n},
             device_id_type=MESH,
-        ).wait_recv()
+        )
+
+    settled(0, count - 1).wait_send()
+    settled(n, radix - 1).wait_recv()
+    for step in range(1, radix):
+        settled(lax.rem(n + step, radix), radix).wait_recv()
 
 
 def finish_kernel(radix, recv, lane_hi, lane_lo, row_hi, row_lo, out_hbm, marg_hbm, fin, prob, marg, sems):
@@ -369,7 +448,7 @@
         return None
     offset = ((layers - 1) * high_bits) % total_bits
     start = offset // 2 - high_bits // 2
-    if layers * radix > LANES or start < 2 or offset // 2 >= pairs or 2 * radix**start != LANES:
+    if layers & (layers - 1) or LANES % (layers * radix) or start < 2 or offset // 2 >= pairs or 2 * radix**start != LANES:
         return None
     rows_hi = radix ** (pairs - offset // 2)
     if rows_hi % 8:
@@ -408,8 +487,9 @@
             pltpu.VMEM(g.shape, f32),
             pltpu.VMEM((count, message, LANES), f32),
             pltpu.SemaphoreType.DMA((2,)),
-            pltpu.SemaphoreType.DMA((count,)),
-            pltpu.SemaphoreType.DMA((count,)),
+            pltpu.SemaphoreType.DMA,
+            pltpu.SemaphoreType.DMA((radix,)),
+            pltpu.SemaphoreType.REGULAR((radix,)),
         ],
         compiler_params=pltpu.CompilerParams(
             collective_id=0, has_side_effects=True, vmem_limit_bytes=8 * 2**20

time: 13.9 us -> 12.6 us (0.906)
  Pallas kernels: 13.1 us -> 11.8 us
    pallas_call x1, Pallas kernels: 11.8 us -> 10.6 us  [merged_local(): pl.pallas_call(functools.partial(exchange_kernel, plan), out_shape=shared...]
where the time goes in v1:
time: 12.6 us; the launch traced here: 12.4 us
  Pallas kernels  11.8 us (94%)
  between operations  0.64 us (5%)
    pallas_call x1, Pallas kernels, merged_local(): pl.pallas_call(functools.partial(exchange_kernel, plan), out_shape=shared...  10.6 us
    pallas_call x1, Pallas kernels, merged_local(): pl.pallas_call(functools.partial(finish_kernel, radix), out_shape=(pltpu....  1.24 us

profile of v1, /device:TPU:0, one launch (start us, length us, event | category | flops | bytes accessed | tf_op | source)
XLA Modules:
  0.0 12.4 jit_solution(9073638458668041626)
XLA Ops:
  0.6 10.6 %exchange.1 = (f32[16,28,128]{2,1,0:T(8,128)S(1)}, bf16[2,128,128]{2,1,0:T(8,128)(2,1)S(1)}, bf16[2,128,128]{2,1,0:T(8,128)(2,1)S(1)}, bf16[2,256,256]{2,1,0:T(8,128)(2,1)S(1)}, bf16[2,256,256]{2,1,0:T(8,128)(2,1)S(1)}) custom-call(f32[256,128]{1,0:T(8,128)} %bitcast.14, f32[56,4,8]{2,1,0:T(4,128)} %bitcast.15), custom_call_target="tpu_custom_call" | custom-call | tf_op jit(solution)/shard_map/exchange/pallas_call | solution.py:480
  11.2 1.2 %finish.1 = (f32[256,128]{1,0:T(8,128)}, f32[32,128]{1,0:T(8,128)}) custom-call(f32[16,28,128]{2,1,0:T(8,128)S(1)} %get-tuple-element.9.recv, bf16[2,128,128]{2,1,0:T(8,128)(2,1)S(1)} %get-tuple-element.10.lane_hi, bf16[2,128,128]{2,1,0:T(8,128)(2,1)S(1)} %get-tuple-element.11.lane_lo, bf16[2,256,256]{2,1,0:T(8,128)(2,1)S(1)} %get-tuple-element.12.row_hi, ...), custom_call_target="tpu_custom_call" | custom-call | tf_op jit(solution)/shard_map/finish/pallas_call | solution.py:502

commit v2 on v1

--- a/solution.py
+++ b/solution.py
@@ -66,55 +66,68 @@
     )
 
 
-def merged_gates(g, plan, order):
+def take_lanes(value, source):
+    return jnp.take_along_axis(value, source, axis=1, mode="promise_in_bounds")
+
+
+def gate_tools(g, plan):
     layers, pairs, shift, total_pairs, _, radix = plan
     shape = (2 * radix, LANES)
     lane = lax.broadcasted_iota(jnp.int32, shape, 1)
     down = lax.broadcasted_iota(jnp.int32, shape, 0)
-    slots = LANES // (radix * layers)
-    layer, row, slot = lane % layers, (lane // layers) % radix, lane // (radix * layers)
+    width = radix * layers
+    layer, row, slot = lane % layers, (lane // layers) % radix, lane // width
     pad = jnp.zeros((radix, LANES - layers), jnp.float32)
-    planes = []
+    tiles, planes = [], []
     for pair in range(pairs):
+        tiles.append([])
         plane = None
         for at in range(radix):
             tile = jnp.concatenate(
                 [jnp.concatenate([g[(pair * 2 + c) * radix + at], pad], axis=1) for c in range(2)], axis=0
             )
-            tile = jnp.take_along_axis(tile, layer, axis=1, mode="promise_in_bounds")
+            tiles[-1].append(tile)
+            tile = take_lanes(tile, layer)
             plane = tile if plane is None else jnp.where(row == at, tile, plane)
         planes.append(plane)
-    unit = jnp.where(down == row, 1.0, 0.0)
     sign = jnp.where(down < radix, -1.0, 1.0)
-    found = {}
-    for begin in range(0, len(order), slots):
-        held = order[begin : begin + slots]
+
+    def merge(held, direct=False):
         place = held[0] - shift * layer
         for index, pair in enumerate(held[1:]):
             place = jnp.where(slot == index + 1, pair - shift * layer, place)
         for _ in range(-(-layers * shift // total_pairs)):
             place = jnp.where(place < 0, place + total_pairs, place)
-        total = unit
+        total = jnp.where(down == row, 1.0, 0.0)
         for pair in range(pairs):
             total = jnp.where(place == pair, planes[pair], total)
         step = 1
         while step < layers:
-            source = slot * (radix * layers) + jnp.maximum(layer - step, 0)
+            before = jnp.maximum(layer - step, 0)
             straight, crossed = None, None
             for at in range(radix):
-                early = jnp.take_along_axis(total, source + at * layers, axis=1, mode="promise_in_bounds")
-                one = total[at : at + 1] * early
-                two = total[radix + at : radix + at + 1] * early
-                straight = one if straight is None else straight + one
-                crossed = two if crossed is None else crossed + two
+                if direct and step == 1:
+                    early = jnp.where(down == at, 1.0, 0.0)
+                    previous = jnp.where(place + shift < total_pairs, place + shift, place + shift - total_pairs)
+                    for pair in range(pairs):
+                        early = jnp.where(previous == pair, take_lanes(tiles[pair][at], before), early)
+                else:
+                    early = take_lanes(total, slot * width + at * layers + before)
+                one_part = total[at : at + 1] * early
+                two_part = total[radix + at : radix + at + 1] * early
+                straight = one_part if straight is None else straight + one_part
+                crossed = two_part if crossed is None else crossed + two_part
             total = straight + sign * pltpu.roll(crossed, radix, 0)
             step *= 2
-        for index, pair in enumerate(held):
-            found[pair] = [
-                jnp.broadcast_to(total[:, at : at + 1], shape)
-                for at in range(index * radix * layers + layers - 1, (index + 1) * radix * layers, layers)
+        return {
+            pair: [
+                take_lanes(total, jnp.full(shape, index * width + (at + 1) * layers - 1, jnp.int32))
+                for at in range(radix)
             ]
-    return found
+            for index, pair in enumerate(held)
+        }
+
+    return merge
 
 
 def kron_all(members):
@@ -173,21 +186,39 @@
     row, core = lax.div(w, 2), lax.rem(w, 2)
     other = 2 * (1 - row)
     seats = [other + core, other + 1 - core, 2 * row + 1 - core, w]
-    for level in range(radix):
-        @pl.when(level >= n)
+    for level in range(1, radix):
+        @pl.when(level > n)
         def _():
-            for seat in seats[:-1]:
+            for seat in range(radix):
                 greet(barrier, seat, level)
 
-            @pl.when(level != n)
-            def _():
-                greet(barrier, w, level)
+    for seat in range(1, radix):
+        @pl.when(seat > w)
+        def _():
+            greet(barrier, seat, n)
+
+    @pl.when(me > 0)
+    def _():
+        pl.semaphore_wait(barrier, me)
+
+    for level in range(radix - 1):
+        @pl.when(level < n)
+        def _():
+            for seat in range(radix):
+                greet(known.at[n], seat, level)
+
+    for seat in range(radix - 1):
+        @pl.when(seat < w)
+        def _():
+            greet(known.at[n], seat, n)
 
     copy_g.wait()
     copy_x.wait()
 
+    merge = gate_tools(g, plan)
     order = list(range(start - 1, start + 2)) + list(range(start - 1)) + list(range(start + 2, total_pairs))
-    gate = merged_gates(g, plan, order)
+    slots = LANES // (radix * layers)
+    gate = merge(order[:slots], True)
     split_gate, low_gate, high_gate = (gate[pair] for pair in range(start - 1, start + 2))
 
     half = LANES // 2
@@ -266,87 +297,102 @@
             blocks.append(pair)
         return blocks
 
-    def put(out_high, held, blocks, take):
+    def put_main(out_high, held, take):
         real, imag = held[take // 2]
         if take % 2:
             main = jnp.where(first, roll(real, half), imag)
         else:
             main = jnp.where(first, real, roll(imag, half))
         send[out_high * radix + take, :rows_hi] = main
+
+    def put_extra(out_high, blocks, take):
         block = None
         for f in range(radix):
             re, im = mixers[take][f]
             term = re * blocks[f][0] + im * blocks[f][1]
             block = term if block is None else block + term
-        spare = (take % 2) * 2 + take // 2
-        if spare != radix - 1:
-            block = jnp.where(outer == spare, roll(block, 2 * group * (spare + 1)), block)
-        moved = [roll(block[rows_hi - tail :], -2 * group * (k + 1)) for k in range(radix - 1)]
+        own = (take % 2) * 2 + take // 2
+        moved = [roll(block[rows_hi - tail :], 2 * group * (own - k)) for k in range(radix) if k != own]
         send[out_high * radix + take, rows_hi:] = jnp.where(
-            outer[: rows_hi - tail] == radix - 1,
-            jnp.concatenate(moved, axis=0),
-            block[: rows_hi - tail],
+            outer[: rows_hi - tail] == own, jnp.concatenate(moved, axis=0), block[: rows_hi - tail]
         )
 
-    def post(seat, level):
+    def post(seat, level, rows):
         pltpu.make_async_remote_copy(
-            src_ref=send.at[seat * radix + level],
-            dst_ref=recv.at[me],
+            src_ref=send.at[seat * radix + level, rows],
+            dst_ref=recv.at[me, rows],
             send_sem=send_sem,
             recv_sem=recv_sem.at[n],
             device_id={"wide": seat, "narrow": level},
             device_id_type=MESH,
         ).start()
 
-    def lowest(seat):
-        @pl.when((n > 0) | (w != seat))
-        def _():
-            post(seat, 0)
+    def lowest(first_seat, rows):
+        last_seat = first_seat + 1
+        alone = (n == 0) & (lax.div(w, 2) == first_seat // 2)
+        other_seat = first_seat + last_seat - w
+
+        def body(seat, carry):
+            post(seat, 0, rows)
+            return carry
+
+        lax.fori_loop(
+            jnp.where(alone, other_seat, first_seat), jnp.where(alone, other_seat, last_seat) + 1, body, 0
+        )
+
+    whole = pl.ds(0, rows_all)
 
     def below(level, carry):
         for seat in seats:
-            post(seat, level)
+            post(seat, level, whole)
         return carry
 
     def above(level, carry):
-        pl.semaphore_wait(known.at[level], 1)
+        pl.semaphore_wait(known.at[level], radix)
         return below(level, carry)
 
-    early = {}
+    early, opened = {}, {}
     for out_high in range(2):
-        held = merged(out_high)
-        early[out_high] = held, transposed(held)
-        put(out_high, *early[out_high], 0)
-
-    pl.semaphore_wait(barrier, radix * (n + 1) - 1)
-    for seat in range(2):
-        lowest(seat)
-    for level in range(radix - 1):
-        @pl.when(n > level)
-        def _():
-            greet(known.at[n], w, level)
+        early[out_high] = merged(out_high)
+        put_main(out_high, early[out_high], 0)
+        opened[out_high] = transposed(early[out_high])
+        put_extra(out_high, opened[out_high], 0)
+
+    peers = radix - 1 - w
+
+    @pl.when((n == 0) & (peers > 0))
+    def _():
+        pl.semaphore_wait(known.at[n], peers)
+
+    lowest(0, whole)
 
     for out_high in (2, 3, 0, 1):
         if out_high in early:
-            held, blocks = early[out_high]
+            held, blocks = early[out_high], opened[out_high]
         else:
             held = merged(out_high)
             blocks = transposed(held)
         for take in range(1 if out_high in early else 0, radix):
-            put(out_high, held, blocks, take)
-
-    for seat in range(2, radix):
-        lowest(seat)
+            put_main(out_high, held, take)
+            put_extra(out_high, blocks, take)
+
+    lowest(2, whole)
     lax.fori_loop(1, n, below, 0)
 
     @pl.when(n > 0)
     def _():
+        @pl.when(peers > 0)
+        def _():
+            pl.semaphore_wait(known.at[n], peers)
+
         for seat in seats[:-1]:
-            post(seat, n)
+            post(seat, n, whole)
 
     lax.fori_loop(n + 1, radix, above, 0)
     recv[me] = send[w * radix + n]
 
+    for begin in range(slots, total_pairs, slots):
+        gate.update(merge(order[begin : begin + slots]))
     low = kron_all([gate[pair] for pair in range(start - 2, -1, -1)])
     block = jnp.concatenate(
         [jnp.concatenate([low[0], low[1]], axis=1), jnp.concatenate([-low[1], low[0]], axis=1)], axis=0
@@ -415,20 +461,22 @@
         prob[index] = density[index * group : (index + 1) * group]
     packed = recv[:, rows_hi:]
     outer = lax.broadcasted_iota(jnp.int32, (1, tail, LANES), 2) // (2 * group)
-    last = None
+    n = lax.axis_index("narrow")
+    own = (n % 2) * 2 + n // 2
+    last = packed[:, :tail]
     for index in range(radix - 1):
+        kept = index + jnp.where(own <= index, 1, 0)
         piece = packed[:, index * tail : (index + 1) * tail]
-        piece = pltpu.roll(piece, 2 * group * (index + 1), 2)
-        last = piece if last is None else jnp.where(outer == index, piece, last)
+        piece = pltpu.roll(piece, lax.rem(2 * group * (kept - own) + LANES, LANES), 2)
+        last = jnp.where(outer == kept, piece, last)
     wide = jnp.concatenate([packed, last], axis=1)
-    with_real, with_imag = apply(1, wide, LANES - 2 * group)
-    total = prob[lax.axis_index("narrow")]
-    for index in range(radix - 1):
+    with_real, with_imag = apply(1, wide, LANES)
+    total = prob[n]
+    for index in range(radix):
         at = 2 * group * index
         real = with_real[at : at + group] - with_imag[at + group : at + 2 * group]
         imag = with_real[at + group : at + 2 * group] + with_imag[at : at + group]
-        term = real * real + imag * imag
-        total = total + term
+        total = total + jnp.where(own == index, 0.0, real * real + imag * imag)
     for block in range(blocks):
         marg[pl.ds(block, group, stride=blocks), :] = total[:, block * LANES : (block + 1) * LANES]
     marg_copy = pltpu.make_async_copy(marg, marg_hbm, sems.at[1])
@@ -448,7 +496,7 @@
         return None
     offset = ((layers - 1) * high_bits) % total_bits
     start = offset // 2 - high_bits // 2
-    if layers & (layers - 1) or LANES % (layers * radix) or start < 2 or offset // 2 >= pairs or 2 * radix**start != LANES:
+    if layers & (layers - 1) or LANES % (layers * radix) or start < 2 or LANES < 3 * layers * radix or offset // 2 >= pairs or 2 * radix**start != LANES:
         return None
     rows_hi = radix ** (pairs - offset // 2)
     if rows_hi % 8:

time: 12.6 us -> 12.3 us (0.976)
  Pallas kernels: 11.8 us -> 11.6 us
    pallas_call x1, Pallas kernels: 10.6 us -> 10.3 us  [merged_local(): pl.pallas_call(functools.partial(exchange_kernel, plan), out_shape=shared...]
where the time goes in v2:
time: 12.3 us; the launch traced here: 12.2 us
  Pallas kernels  11.6 us (94%)
  between operations  0.64 us (5%)
    pallas_call x1, Pallas kernels, merged_local(): pl.pallas_call(functools.partial(exchange_kernel, plan), out_shape=shared...  10.3 us
    pallas_call x1, Pallas kernels, merged_local(): pl.pallas_call(functools.partial(finish_kernel, radix), out_shape=(pltpu....  1.29 us

profile of v2, /device:TPU:0, one launch (start us, length us, event | category | flops | bytes accessed | tf_op | source)
XLA Modules:
  0.0 12.2 jit_solution(7446851402553002301)
XLA Ops:
  0.6 10.3 %exchange.1 = (f32[16,28,128]{2,1,0:T(8,128)S(1)}, bf16[2,128,128]{2,1,0:T(8,128)(2,1)S(1)}, bf16[2,128,128]{2,1,0:T(8,128)(2,1)S(1)}, bf16[2,256,256]{2,1,0:T(8,128)(2,1)S(1)}, bf16[2,256,256]{2,1,0:T(8,128)(2,1)S(1)}) custom-call(f32[256,128]{1,0:T(8,128)} %bitcast.14, f32[56,4,8]{2,1,0:T(4,128)} %bitcast.15), custom_call_target="tpu_custom_call" | custom-call | tf_op jit(solution)/shard_map/exchange/pallas_call | solution.py:528
  10.9 1.3 %finish.1 = (f32[256,128]{1,0:T(8,128)}, f32[32,128]{1,0:T(8,128)}) custom-call(f32[16,28,128]{2,1,0:T(8,128)S(1)} %get-tuple-element.9.recv, bf16[2,128,128]{2,1,0:T(8,128)(2,1)S(1)} %get-tuple-element.10.lane_hi, bf16[2,128,128]{2,1,0:T(8,128)(2,1)S(1)} %get-tuple-element.11.lane_lo, bf16[2,256,256]{2,1,0:T(8,128)(2,1)S(1)} %get-tuple-element.12.row_hi, ...), custom_call_target="tpu_custom_call" | custom-call | tf_op jit(solution)/shard_map/finish/pallas_call | solution.py:550

commit v3 on v2

--- a/solution.py
+++ b/solution.py
@@ -376,11 +376,7 @@
             put_main(out_high, held, take)
             put_extra(out_high, blocks, take)
 
-    lowest(2, whole)
-    lax.fori_loop(1, n, below, 0)
-
-    @pl.when(n > 0)
-    def _():
+    def own_level():
         @pl.when(peers > 0)
         def _():
             pl.semaphore_wait(known.at[n], peers)
@@ -388,7 +384,20 @@
         for seat in seats[:-1]:
             post(seat, n, whole)
 
-    lax.fori_loop(n + 1, radix, above, 0)
+    lowest(2, whole)
+
+    @pl.when(n == 2)
+    def _():
+        own_level()
+        above(3, 0)
+
+    lax.fori_loop(1, n, below, 0)
+
+    @pl.when((n == 1) | (n == 3))
+    def _():
+        own_level()
+
+    lax.fori_loop(jnp.where(n == 2, radix, n + 1), radix, above, 0)
     recv[me] = send[w * radix + n]
 
     for begin in range(slots, total_pairs, slots):

time: 12.3 us -> 12 us (0.976)
  the two profiles are of different devices: /device:TPU:0 before, /device:TPU:27 now
where the time goes in v3:
time: 12 us; the launch traced here: 11.8 us
  Pallas kernels  11.2 us (93%)
  between operations  0.64 us (5%)
    pallas_call x1, Pallas kernels, merged_local(): pl.pallas_call(functools.partial(exchange_kernel, plan), out_shape=shared...  9.89 us
    pallas_call x1, Pallas kernels, merged_local(): pl.pallas_call(functools.partial(finish_kernel, radix), out_shape=(pltpu....  1.29 us

profile of v3, /device:TPU:27, one launch (start us, length us, event | category | flops | bytes accessed | tf_op | source)
XLA Modules:
  0.0 11.8 jit_solution(6797809367976493090)
XLA Ops:
  0.6 9.9 %exchange.1 = (f32[16,28,128]{2,1,0:T(8,128)S(1)}, bf16[2,128,128]{2,1,0:T(8,128)(2,1)S(1)}, bf16[2,128,128]{2,1,0:T(8,128)(2,1)S(1)}, bf16[2,256,256]{2,1,0:T(8,128)(2,1)S(1)}, bf16[2,256,256]{2,1,0:T(8,128)(2,1)S(1)}) custom-call(f32[256,128]{1,0:T(8,128)} %bitcast.14, f32[56,4,8]{2,1,0:T(4,128)} %bitcast.15), custom_call_target="tpu_custom_call" | custom-call | tf_op jit(solution)/shard_map/exchange/pallas_call | solution.py:537
  10.5 1.3 %finish.1 = (f32[256,128]{1,0:T(8,128)}, f32[32,128]{1,0:T(8,128)}) custom-call(f32[16,28,128]{2,1,0:T(8,128)S(1)} %get-tuple-element.9.recv, bf16[2,128,128]{2,1,0:T(8,128)(2,1)S(1)} %get-tuple-element.10.lane_hi, bf16[2,128,128]{2,1,0:T(8,128)(2,1)S(1)} %get-tuple-element.11.lane_lo, bf16[2,256,256]{2,1,0:T(8,128)(2,1)S(1)} %get-tuple-element.12.row_hi, ...), custom_call_target="tpu_custom_call" | custom-call | tf_op jit(solution)/shard_map/finish/pallas_call | solution.py:559

commit v4 on v3

--- a/solution.py
+++ b/solution.py
@@ -159,18 +159,55 @@
     return high, (value - high.astype(jnp.float32)).astype(jnp.bfloat16)
 
 
-def dot(left, right, contract):
+def precise(left, right, contract):
     def one(a, b):
         return lax.dot_general(a, b, (((1,), (contract,)), ((), ())), preferred_element_type=jnp.float32)
 
     return one(left[0], right[0]) + (one(left[0], right[1]) + one(left[1], right[0]))
 
 
+def precise_one(a, b):
+    return lax.dot_general(a, b, (((1,), (0,)), ((), ())), preferred_element_type=jnp.float32)
+
+
+def pairs_of(n):
+    near = n, jnp.where(n == 0, 1, n - 1)
+    return near, (jnp.where(n < 2, 2, 0), jnp.where(n < 3, 3, 1))
+
+
+def contribution(radix, recv, lanes, rows, levels, n):
+    held = jnp.concatenate([recv[pl.ds(level * radix, radix)] for level in levels], axis=0)
+    rows_hi = held.shape[1] * radix // (2 * radix - 1)
+    tail = rows_hi // radix
+    size = held.shape[0] * rows_hi
+    wide = LANES // radix
+    packed = held[:, rows_hi:]
+    outer = lax.broadcasted_iota(jnp.int32, (1, tail, LANES), 2) // wide
+    own = (n % 2) * 2 + n // 2
+    last = packed[:, :tail]
+    for index in range(radix - 1):
+        kept = index + jnp.where(own <= index, 1, 0)
+        piece = packed[:, index * tail : (index + 1) * tail]
+        piece = pltpu.roll(piece, lax.rem(wide * (kept - own) + LANES, LANES), 2)
+        last = jnp.where(outer == kept, piece, last)
+    turned = []
+    for which, value in enumerate((held[:, :rows_hi], jnp.concatenate([packed, last], axis=1))):
+        item = precise(tuple(part[which] for part in lanes), split(value.reshape(size, LANES)), 1)
+        turned.append(jnp.concatenate([item[: LANES // 2], item[LANES // 2 :]], axis=1))
+    matrix = [
+        jnp.concatenate([part[c, level] for c in range(2) for level in levels], axis=0) for part in rows
+    ]
+    high, low = split(jnp.concatenate(turned, axis=0))
+    both = precise_one(jnp.concatenate([high, low], axis=0), matrix[0])
+    rows = high.shape[0]
+    return both[:rows] + (both[rows:] + precise_one(high, matrix[1]))
+
+
 def greet(semaphore, seat, level):
     pl.semaphore_signal(semaphore, inc=1, device_id={"wide": seat, "narrow": level}, device_id_type=MESH)
 
 
-def exchange_kernel(plan, x_hbm, g_hbm, recv, lane_hi, lane_lo, row_hi, row_lo, x, g, send,
+def exchange_kernel(plan, x_hbm, g_hbm, recv, acc, lane_hi, lane_lo, row_hi, row_lo, x, g, send,
                     local_sem, send_sem, recv_sem, known):
     layers, pairs, shift, total_pairs, start, radix = plan
     w = lax.axis_index("wide")
@@ -186,31 +223,31 @@
     row, core = lax.div(w, 2), lax.rem(w, 2)
     other = 2 * (1 - row)
     seats = [other + core, other + 1 - core, 2 * row + 1 - core, w]
+    for seat in range(1, radix):
+        @pl.when(seat > w)
+        def _():
+            greet(barrier, seat, n)
+
     for level in range(1, radix):
         @pl.when(level > n)
         def _():
             for seat in range(radix):
                 greet(barrier, seat, level)
 
-    for seat in range(1, radix):
-        @pl.when(seat > w)
-        def _():
-            greet(barrier, seat, n)
-
     @pl.when(me > 0)
     def _():
         pl.semaphore_wait(barrier, me)
 
-    for level in range(radix - 1):
+    for level in range(radix - 2, -1, -1):
         @pl.when(level < n)
         def _():
             for seat in range(radix):
-                greet(known.at[n], seat, level)
+                greet(known.at[n, row], seat, level)
 
     for seat in range(radix - 1):
         @pl.when(seat < w)
         def _():
-            greet(known.at[n], seat, n)
+            greet(known.at[n, row], seat, n)
 
     copy_g.wait()
     copy_x.wait()
@@ -348,8 +385,11 @@
         return carry
 
     def above(level, carry):
-        pl.semaphore_wait(known.at[level], radix)
-        return below(level, carry)
+        for side, pair in ((row, seats[2:]), (1 - row, seats[:2])):
+            pl.semaphore_wait(known.at[level, side], 2)
+            for seat in pair:
+                post(seat, level, whole)
+        return carry
 
     early, opened = {}, {}
     for out_high in range(2):
@@ -358,11 +398,19 @@
         opened[out_high] = transposed(early[out_high])
         put_extra(out_high, opened[out_high], 0)
 
-    peers = radix - 1 - w
-
-    @pl.when((n == 0) & (peers > 0))
+    def meet():
+        @pl.when(core == 0)
+        def _():
+            pl.semaphore_wait(known.at[n, row], 1)
+
+        @pl.when(row == 0)
+        def _():
+            pl.semaphore_wait(known.at[n, 1], 2)
+
+
+    @pl.when(n == 0)
     def _():
-        pl.semaphore_wait(known.at[n], peers)
+        meet()
 
     lowest(0, whole)
 
@@ -377,10 +425,7 @@
             put_extra(out_high, blocks, take)
 
     def own_level():
-        @pl.when(peers > 0)
-        def _():
-            pl.semaphore_wait(known.at[n], peers)
-
+        meet()
         for seat in seats[:-1]:
             post(seat, n, whole)
 
@@ -415,15 +460,21 @@
         [jnp.concatenate([parts[0], parts[1]], axis=1), jnp.concatenate([-parts[1], parts[0]], axis=1)],
         axis=0,
     ).T
+    stripes = range(0, LANES, 2 * group)
+    grouped = jnp.concatenate(
+        [grouped[at + shift : at + shift + group] for shift in (0, group) for at in stripes], axis=0
+    )
     for index, item in enumerate((plain, grouped)):
         lane_hi[index], lane_lo[index] = split(item)
     row_members = [gate[pair] for pair in range(total_pairs - 1, start + 1, -1)]
-    for index, item in enumerate(kron_all(row_members)):
-        for at, held in enumerate(split(item)):
-            into = (row_hi, row_lo)[at]
-            for source in range(count):
-                place = (source % radix) * radix + source // radix
-                into[index, place * rows_hi : (place + 1) * rows_hi] = held[source * rows_hi : (source + 1) * rows_hi]
+    real, imag = (split(item) for item in kron_all(row_members))
+    for at, into in enumerate((row_hi, row_lo)):
+        for source in range(count):
+            seat, level = source // radix, source % radix
+            rows = slice(source * rows_hi, (source + 1) * rows_hi)
+            place = slice(seat * rows_hi, (seat + 1) * rows_hi)
+            into[0, level, place] = jnp.concatenate([real[at][rows], imag[at][rows]], axis=1)
+            into[1, level, place] = jnp.concatenate([-imag[at][rows], real[at][rows]], axis=1)
 
     def settled(group, size):
         return pltpu.make_async_remote_copy(
@@ -435,57 +486,37 @@
             device_id_type=MESH,
         )
 
+    near, far = pairs_of(n)
+    settled(near[0], radix - 1).wait_recv()
+    settled(near[1], radix).wait_recv()
+    acc[...] = contribution(radix, recv, (lane_hi, lane_lo), (row_hi, row_lo), near, n)
     settled(0, count - 1).wait_send()
-    settled(n, radix - 1).wait_recv()
-    for step in range(1, radix):
-        settled(lax.rem(n + step, radix), radix).wait_recv()
-
-
-def finish_kernel(radix, recv, lane_hi, lane_lo, row_hi, row_lo, out_hbm, marg_hbm, fin, prob, marg, sems):
-    rows_hi = recv.shape[1] * radix // (2 * radix - 1)
-    tail = rows_hi // radix
-    size = recv.shape[0] * rows_hi
+    for level in far:
+        settled(level, radix).wait_recv()
+
+
+def finish_kernel(radix, recv, acc, lane_hi, lane_lo, row_hi, row_lo, out_hbm, marg_hbm, fin, prob, marg, sems):
     half = LANES // 2
     group = half // radix
+    size = acc.shape[1] // 2
     blocks = size // LANES
-    rows = (row_hi[0], row_lo[0]), (row_hi[1], row_lo[1])
-
-    def apply(which, value, keep):
-        held = split(value.reshape(size, LANES))
-        turned = dot((lane_hi[which], lane_lo[which]), held, 1)
-        turned = split(turned[:keep])
-        return dot(turned, rows[0], 0), dot(turned, rows[1], 0)
-
-    with_real, with_imag = apply(0, recv[:, :rows_hi], LANES)
-    real = with_real[:half] - with_imag[half:]
-    imag = with_real[half:] + with_imag[:half]
+    n = lax.axis_index("narrow")
+    own = (n % 2) * 2 + n // 2
+    total = acc[...] + contribution(radix, recv, (lane_hi, lane_lo), (row_hi, row_lo), pairs_of(n)[1], n)
+    real, imag = total[:, :size], total[:, size:]
     for block in range(blocks):
         columns = slice(block * LANES, (block + 1) * LANES)
-        fin[pl.ds(block * 2, half, stride=2 * blocks), :] = real[:, columns]
-        fin[pl.ds(block * 2 + 1, half, stride=2 * blocks), :] = imag[:, columns]
+        fin[pl.ds(block * 2, half, stride=2 * blocks), :] = real[:half, columns]
+        fin[pl.ds(block * 2 + 1, half, stride=2 * blocks), :] = imag[:half, columns]
     out_copy = pltpu.make_async_copy(fin, out_hbm, sems.at[0])
     out_copy.start()
     density = real * real + imag * imag
     for index in range(radix):
         prob[index] = density[index * group : (index + 1) * group]
-    packed = recv[:, rows_hi:]
-    outer = lax.broadcasted_iota(jnp.int32, (1, tail, LANES), 2) // (2 * group)
-    n = lax.axis_index("narrow")
-    own = (n % 2) * 2 + n // 2
-    last = packed[:, :tail]
-    for index in range(radix - 1):
-        kept = index + jnp.where(own <= index, 1, 0)
-        piece = packed[:, index * tail : (index + 1) * tail]
-        piece = pltpu.roll(piece, lax.rem(2 * group * (kept - own) + LANES, LANES), 2)
-        last = jnp.where(outer == kept, piece, last)
-    wide = jnp.concatenate([packed, last], axis=1)
-    with_real, with_imag = apply(1, wide, LANES)
     total = prob[n]
     for index in range(radix):
-        at = 2 * group * index
-        real = with_real[at : at + group] - with_imag[at + group : at + 2 * group]
-        imag = with_real[at + group : at + 2 * group] + with_imag[at : at + group]
-        total = total + jnp.where(own == index, 0.0, real * real + imag * imag)
+        at = half + group * index
+        total = total + jnp.where(own == index, 0.0, density[at : at + group])
     for block in range(blocks):
         marg[pl.ds(block, group, stride=blocks), :] = total[:, block * LANES : (block + 1) * LANES]
     marg_copy = pltpu.make_async_copy(marg, marg_hbm, sems.at[1])
@@ -529,10 +560,11 @@
     message = 2 * rows_hi - rows_hi // radix
     shared = (
         pltpu.VMEM((count, message, LANES), f32),
+        pltpu.VMEM((LANES, 2 * size), f32),
         pltpu.VMEM((2, LANES, LANES), bf16),
         pltpu.VMEM((2, LANES, LANES), bf16),
-        pltpu.VMEM((2, size, size), bf16),
-        pltpu.VMEM((2, size, size), bf16),
+        pltpu.VMEM((2, radix, size // radix, 2 * size), bf16),
+        pltpu.VMEM((2, radix, size // radix, 2 * size), bf16),
     )
     held = pl.pallas_call(
         functools.partial(exchange_kernel, plan),
@@ -546,7 +578,7 @@
             pltpu.SemaphoreType.DMA((2,)),
             pltpu.SemaphoreType.DMA,
             pltpu.SemaphoreType.DMA((radix,)),
-            pltpu.SemaphoreType.REGULAR((radix,)),
+            pltpu.SemaphoreType.REGULAR((radix, 2)),
         ],
         compiler_params=pltpu.CompilerParams(
             collective_id=0, has_side_effects=True, vmem_limit_bytes=8 * 2**20

time: 12 us -> 11.8 us (0.983)
  the two profiles are of different devices: /device:TPU:27 before, /device:TPU:9 now
where the time goes in v4:
time: 11.8 us; the launch traced here: 11.7 us
  Pallas kernels  11.1 us (94%)
  between operations  0.64 us (5%)
    pallas_call x1, Pallas kernels, merged_local(): pl.pallas_call(functools.partial(exchange_kernel, plan), out_shape=shared...  9.84 us
    pallas_call x1, Pallas kernels, merged_local(): pl.pallas_call(functools.partial(finish_kernel, radix), out_shape=(pltpu....  1.21 us

profile of v4, /device:TPU:9, one launch (start us, length us, event | category | flops | bytes accessed | tf_op | source)
XLA Modules:
  0.0 11.7 jit_solution(14115473479141500868)
XLA Ops:
  0.6 9.8 %exchange.1 = (f32[16,28,128]{2,1,0:T(8,128)S(1)}, f32[128,512]{1,0:T(8,128)S(1)}, bf16[2,128,128]{2,1,0:T(8,128)(2,1)S(1)}, bf16[2,128,128]{2,1,0:T(8,128)(2,1)...) custom-call(f32[256,128]{1,0:T(8,128)} %bitcast.14, f32[56,4,8]{2,1,0:T(4,128)} %bitcast.15), custom_call_target="tpu_custom_call" | custom-call | tf_op jit(solution)/shard_map/exchange/pallas_call | solution.py:569
  10.5 1.2 %finish.1 = (f32[256,128]{1,0:T(8,128)}, f32[32,128]{1,0:T(8,128)}) custom-call(f32[16,28,128]{2,1,0:T(8,128)S(1)} %get-tuple-element.10.recv, f32[128,512]{1,0:T(8,128)S(1)} %get-tuple-element.11.acc, bf16[2,128,128]{2,1,0:T(8,128)(2,1)S(1)} %get-tuple-element.12.lane_hi, bf16[2,128,128]{2,1,0:T(8,128)(2,1)S(1)} %get-tuple-element.13.lane_lo, ...), custom_call_target="tpu_custom_call" | custom-call | tf_op jit(solution)/shard_map/finish/pallas_call | solution.py:591

commit v5 on v4

--- a/solution.py
+++ b/solution.py
@@ -286,29 +286,33 @@
 
     same = [[both(low_gate, (2 * o, 2 * i), (2 * o + 1, 2 * i + 1)) for i in range(2)] for o in range(2)]
     cross = [[both(low_gate, (2 * o, 2 * i + 1), (2 * o + 1, 2 * i)) for i in range(2)] for o in range(2)]
-    stage = []
+    helds, stage = [], []
     stride = 4 * radix
     for high in range(radix):
         held = []
         for i in range(2):
             held.append(tuple(x[pl.ds(high * 4 + i * 2 + c, rows_hi, stride=stride), :] for c in range(2)))
-        turned = [tuple(roll(v, half) for v in pair) for pair in held]
-        result = []
-        for o in range(2):
+        helds.append((held, [tuple(roll(v, half) for v in pair) for pair in held]))
+        stage.append([])
+
+    def advance(o):
+        for high in range(radix):
+            held, turned = helds[high]
             total = None
             for i in range(2):
                 total = add(total, complex_mul(same[o][i], held[i]))
                 total = add(total, complex_mul(cross[o][i], turned[i]))
-            result.append(total)
-        stage.append(result)
+            stage[high].append(total)
+
+    advance(0)
     sign = jnp.where(field % 2 == 0, -1.0, 1.0)
     mixers = [[entry(split_gate, take, f) for f in range(radix)] for take in range(radix)]
     mixers = [[(re, im * sign) for re, im in line] for line in mixers]
 
-    def merged(out_high):
+    def merged(out_high, which):
         coefs = [entry(high_gate, out_high, high) for high in range(radix)]
         held = []
-        for o in range(2):
+        for o in which:
             total = None
             for high in range(radix):
                 total = add(total, complex_mul(coefs[high], stage[high][o]))
@@ -393,10 +397,8 @@
 
     early, opened = {}, {}
     for out_high in range(2):
-        early[out_high] = merged(out_high)
+        early[out_high] = merged(out_high, (0,))
         put_main(out_high, early[out_high], 0)
-        opened[out_high] = transposed(early[out_high])
-        put_extra(out_high, opened[out_high], 0)
 
     def meet():
         @pl.when(core == 0)
@@ -412,13 +414,20 @@
     def _():
         meet()
 
-    lowest(0, whole)
+    lowest(0, pl.ds(0, rows_hi))
+    advance(1)
+    for out_high in range(2):
+        early[out_high] += merged(out_high, (1,))
+        opened[out_high] = transposed(early[out_high])
+        put_extra(out_high, opened[out_high], 0)
+
+    lowest(0, pl.ds(rows_hi, rows_all - rows_hi))
 
     for out_high in (2, 3, 0, 1):
         if out_high in early:
             held, blocks = early[out_high], opened[out_high]
         else:
-            held = merged(out_high)
+            held = merged(out_high, (0, 1))
             blocks = transposed(held)
         for take in range(1 if out_high in early else 0, radix):
             put_main(out_high, held, take)

time: 11.8 us -> 11.8 us (level)
  the two profiles are of different devices: /device:TPU:9 before, /device:TPU:27 now
where the time goes in v5:
time: 11.8 us; the launch traced here: 11.7 us
  Pallas kernels  11.1 us (94%)
  between operations  0.64 us (5%)
    pallas_call x1, Pallas kernels, merged_local(): pl.pallas_call(functools.partial(exchange_kernel, plan), out_shape=shared...  9.84 us
    pallas_call x1, Pallas kernels, merged_local(): pl.pallas_call(functools.partial(finish_kernel, radix), out_shape=(pltpu....  1.21 us

profile of v5, /device:TPU:27, one launch (start us, length us, event | category | flops | bytes accessed | tf_op | source)
XLA Modules:
  0.0 11.7 jit_solution(15257413369118299593)
XLA Ops:
  0.6 9.8 %exchange.1 = (f32[16,28,128]{2,1,0:T(8,128)S(1)}, f32[128,512]{1,0:T(8,128)S(1)}, bf16[2,128,128]{2,1,0:T(8,128)(2,1)S(1)}, bf16[2,128,128]{2,1,0:T(8,128)(2,1)...) custom-call(f32[256,128]{1,0:T(8,128)} %bitcast.14, f32[56,4,8]{2,1,0:T(4,128)} %bitcast.15), custom_call_target="tpu_custom_call" | custom-call | tf_op jit(solution)/shard_map/exchange/pallas_call | solution.py:578
  10.5 1.2 %finish.1 = (f32[256,128]{1,0:T(8,128)}, f32[32,128]{1,0:T(8,128)}) custom-call(f32[16,28,128]{2,1,0:T(8,128)S(1)} %get-tuple-element.10.recv, f32[128,512]{1,0:T(8,128)S(1)} %get-tuple-element.11.acc, bf16[2,128,128]{2,1,0:T(8,128)(2,1)S(1)} %get-tuple-element.12.lane_hi, bf16[2,128,128]{2,1,0:T(8,128)(2,1)S(1)} %get-tuple-element.13.lane_lo, ...), custom_call_target="tpu_custom_call" | custom-call | tf_op jit(solution)/shard_map/finish/pallas_call | solution.py:600

commit v6 on v5

--- a/solution.py
+++ b/solution.py
@@ -222,6 +222,7 @@
     copy_x.start()
     row, core = lax.div(w, 2), lax.rem(w, 2)
     other = 2 * (1 - row)
+    ordered = [other + 1, other, 2 * row + 1, 2 * row]
     seats = [other + core, other + 1 - core, 2 * row + 1 - core, w]
     for seat in range(1, radix):
         @pl.when(seat > w)
@@ -389,7 +390,7 @@
         return carry
 
     def above(level, carry):
-        for side, pair in ((row, seats[2:]), (1 - row, seats[:2])):
+        for side, pair in ((row, ordered[2:]), (1 - row, ordered[:2])):
             pl.semaphore_wait(known.at[level, side], 2)
             for seat in pair:
                 post(seat, level, whole)

time: 11.8 us -> 11.7 us (level)
  the two profiles are of different devices: /device:TPU:27 before, /device:TPU:0 now
where the time goes in v6:
time: 11.7 us; the launch traced here: 11.5 us
  Pallas kernels  10.9 us (93%)
  between operations  0.64 us (5%)
    pallas_call x1, Pallas kernels, merged_local(): pl.pallas_call(functools.partial(exchange_kernel, plan), out_shape=shared...  9.68 us
    pallas_call x1, Pallas kernels, merged_local(): pl.pallas_call(functools.partial(finish_kernel, radix), out_shape=(pltpu....  1.21 us

profile of v6, /device:TPU:0, one launch (start us, length us, event | category | flops | bytes accessed | tf_op | source)
XLA Modules:
  0.0 11.5 jit_solution(16199147616789002606)
XLA Ops:
  0.6 9.7 %exchange.1 = (f32[16,28,128]{2,1,0:T(8,128)S(1)}, f32[128,512]{1,0:T(8,128)S(1)}, bf16[2,128,128]{2,1,0:T(8,128)(2,1)S(1)}, bf16[2,128,128]{2,1,0:T(8,128)(2,1)...) custom-call(f32[256,128]{1,0:T(8,128)} %bitcast.14, f32[56,4,8]{2,1,0:T(4,128)} %bitcast.15), custom_call_target="tpu_custom_call" | custom-call | tf_op jit(solution)/shard_map/exchange/pallas_call | solution.py:579
  10.3 1.2 %finish.1 = (f32[256,128]{1,0:T(8,128)}, f32[32,128]{1,0:T(8,128)}) custom-call(f32[16,28,128]{2,1,0:T(8,128)S(1)} %get-tuple-element.10.recv, f32[128,512]{1,0:T(8,128)S(1)} %get-tuple-element.11.acc, bf16[2,128,128]{2,1,0:T(8,128)(2,1)S(1)} %get-tuple-element.12.lane_hi, bf16[2,128,128]{2,1,0:T(8,128)(2,1)S(1)} %get-tuple-element.13.lane_lo, ...), custom_call_target="tpu_custom_call" | custom-call | tf_op jit(solution)/shard_map/finish/pallas_call | solution.py:601

commit v7 on v5

--- a/solution.py
+++ b/solution.py
@@ -222,6 +222,7 @@
     copy_x.start()
     row, core = lax.div(w, 2), lax.rem(w, 2)
     other = 2 * (1 - row)
+    rows_first = [core, 1 - core, 2 + core, 3 - core]
     seats = [other + core, other + 1 - core, 2 * row + 1 - core, w]
     for seat in range(1, radix):
         @pl.when(seat > w)
@@ -384,12 +385,12 @@
     whole = pl.ds(0, rows_all)
 
     def below(level, carry):
-        for seat in seats:
+        for seat in rows_first:
             post(seat, level, whole)
         return carry
 
     def above(level, carry):
-        for side, pair in ((row, seats[2:]), (1 - row, seats[:2])):
+        for side, pair in ((0, (1, 0)), (1, (3, 2))):
             pl.semaphore_wait(known.at[level, side], 2)
             for seat in pair:
                 post(seat, level, whole)

time: 11.8 us -> 11.9 us (level)
  the two profiles are of different devices: /device:TPU:27 before, /device:TPU:26 now
where the time goes in v7:
time: 11.9 us; the launch traced here: 11.8 us
  Pallas kernels  11.2 us (94%)
  between operations  0.64 us (5%)
    pallas_call x1, Pallas kernels, merged_local(): pl.pallas_call(functools.partial(exchange_kernel, plan), out_shape=shared...  9.96 us
    pallas_call x1, Pallas kernels, merged_local(): pl.pallas_call(functools.partial(finish_kernel, radix), out_shape=(pltpu....  1.21 us

profile of v7, /device:TPU:26, one launch (start us, length us, event | category | flops | bytes accessed | tf_op | source)
XLA Modules:
  0.0 11.8 jit_solution(12839456389669631248)
XLA Ops:
  0.6 10.0 %exchange.1 = (f32[16,28,128]{2,1,0:T(8,128)S(1)}, f32[128,512]{1,0:T(8,128)S(1)}, bf16[2,128,128]{2,1,0:T(8,128)(2,1)S(1)}, bf16[2,128,128]{2,1,0:T(8,128)(2,1)...) custom-call(f32[256,128]{1,0:T(8,128)} %bitcast.14, f32[56,4,8]{2,1,0:T(4,128)} %bitcast.15), custom_call_target="tpu_custom_call" | custom-call | tf_op jit(solution)/shard_map/exchange/pallas_call | solution.py:579
  10.6 1.2 %finish.1 = (f32[256,128]{1,0:T(8,128)}, f32[32,128]{1,0:T(8,128)}) custom-call(f32[16,28,128]{2,1,0:T(8,128)S(1)} %get-tuple-element.10.recv, f32[128,512]{1,0:T(8,128)S(1)} %get-tuple-element.11.acc, bf16[2,128,128]{2,1,0:T(8,128)(2,1)S(1)} %get-tuple-element.12.lane_hi, bf16[2,128,128]{2,1,0:T(8,128)(2,1)S(1)} %get-tuple-element.13.lane_lo, ...), custom_call_target="tpu_custom_call" | custom-call | tf_op jit(solution)/shard_map/finish/pallas_call | solution.py:601

commit v8 on v6

--- a/solution.py
+++ b/solution.py
@@ -443,8 +443,8 @@
 
     @pl.when(n == 2)
     def _():
+        above(3, 0)
         own_level()
-        above(3, 0)
 
     lax.fori_loop(1, n, below, 0)
 

time: 11.7 us -> 11.7 us (level)
  no operation moved by 1% of the time
where the time goes in v8:
time: 11.7 us; the launch traced here: 11.5 us
  Pallas kernels  10.9 us (93%)
  between operations  0.64 us (5%)
    pallas_call x1, Pallas kernels, merged_local(): pl.pallas_call(functools.partial(exchange_kernel, plan), out_shape=shared...  9.68 us
    pallas_call x1, Pallas kernels, merged_local(): pl.pallas_call(functools.partial(finish_kernel, radix), out_shape=(pltpu....  1.21 us

profile of v8, /device:TPU:0, one launch (start us, length us, event | category | flops | bytes accessed | tf_op | source)
XLA Modules:
  0.0 11.5 jit_solution(3712944426152559194)
XLA Ops:
  0.6 9.7 %exchange.1 = (f32[16,28,128]{2,1,0:T(8,128)S(1)}, f32[128,512]{1,0:T(8,128)S(1)}, bf16[2,128,128]{2,1,0:T(8,128)(2,1)S(1)}, bf16[2,128,128]{2,1,0:T(8,128)(2,1)...) custom-call(f32[256,128]{1,0:T(8,128)} %bitcast.14, f32[56,4,8]{2,1,0:T(4,128)} %bitcast.15), custom_call_target="tpu_custom_call" | custom-call | tf_op jit(solution)/shard_map/exchange/pallas_call | solution.py:579
  10.3 1.2 %finish.1 = (f32[256,128]{1,0:T(8,128)}, f32[32,128]{1,0:T(8,128)}) custom-call(f32[16,28,128]{2,1,0:T(8,128)S(1)} %get-tuple-element.10.recv, f32[128,512]{1,0:T(8,128)S(1)} %get-tuple-element.11.acc, bf16[2,128,128]{2,1,0:T(8,128)(2,1)S(1)} %get-tuple-element.12.lane_hi, bf16[2,128,128]{2,1,0:T(8,128)(2,1)S(1)} %get-tuple-element.13.lane_lo, ...), custom_call_target="tpu_custom_call" | custom-call | tf_op jit(solution)/shard_map/finish/pallas_call | solution.py:601
